TPU v7x, 16 devices: a 4x2x1 block of a 4x4x8 slice. The times are simulated.
16 devices in a mesh: rep: 2 (over y, z), vocab: 8 (over x, core).
Axes of the slice: x: 4, y: 2, z: 1, core: 2. Of those that a mesh axis runs over, the one named last changes fastest.
The devices are a block of a 4x4x8 slice.
Arguments:
- hidden: bfloat16 [8192, 2304], P(('rep', 'vocab')), parts along dimension 0
- w_head: bfloat16 [256000, 2304], P('vocab')
- allowed_ids: int32 [4096], P('rep'), parts along dimension 0
- allowed_valid: int32 [4096], P('rep'), parts along dimension 0
- target_pos: int32 [8192], P(('rep', 'vocab')), parts along dimension 0
Outputs:
- output 1: float32 [8192, 2048], P(('rep', 'vocab')), parts along dimension 0
- output 2: float32 [8192], P(('rep', 'vocab')), parts along dimension 0
There are 2 independent parts. A program takes and returns all parts, laid end to end along the dimension named above; an argument that names none is the same for every part.
All inputs are finite; a program needn't handle non-finite values.
Results may differ from a plain program's by a relative error of at most 0.001.
Values are sent between devices in bfloat16 or wider.
A program may use at most 768 MiB of HBM per device.

v0:
```python
import jax
import jax.numpy as jnp
from jax import lax
from jax.sharding import PartitionSpec as P

INV_TEMP = 1.25


def owner_layout(allowed_ids, vocab_local, shards, slot_cap, my_index):
    owner_id = allowed_ids // vocab_local
    sort_order = jnp.argsort(owner_id, stable=True)
    counts = jnp.bincount(owner_id, length=shards)
    starts = jnp.cumsum(counts) - counts
    slot_rank = jnp.argsort(sort_order) - starts[owner_id]
    padded = jnp.concatenate([sort_order, jnp.zeros((slot_cap,), sort_order.dtype)])
    mine_pos = lax.dynamic_slice(padded, (starts[my_index],), (slot_cap,))
    local_idx = jnp.clip(allowed_ids[mine_pos] - my_index * vocab_local, 0, vocab_local - 1)
    return owner_id, slot_rank, local_idx


def finish_rows(own_scores, owner_id, slot_rank, allowed_valid, target_pos, shards):
    rows_dev = target_pos.shape[0]
    outgoing = own_scores.reshape(shards, rows_dev, own_scores.shape[1])
    incoming = lax.all_to_all(outgoing, 'vocab', 0, 0)
    scores = incoming[owner_id, :, slot_rank].T
    keep_mask = (allowed_valid > 0)[None, :]
    masked = jnp.where(keep_mask, scores, -jnp.inf)
    log_norm = jax.nn.logsumexp(masked, axis=1)
    token_probs = jnp.where(keep_mask, jnp.exp(masked - log_norm[:, None]), 0.0)
    picked = jnp.take_along_axis(scores, target_pos[:, None], axis=1)[:, 0]
    return token_probs, picked - log_norm


def solution(mesh):
    shards = mesh.shape['vocab']

    def device_step(hidden, w_head, allowed_ids, allowed_valid, target_pos):
        my_index = lax.axis_index('vocab')
        vocab_local = w_head.shape[0]
        slot_cap = 2 * allowed_ids.shape[0] // shards
        owner_id, slot_rank, local_idx = owner_layout(allowed_ids, vocab_local, shards, slot_cap, my_index)
        mine_rows = jnp.take(w_head, local_idx, axis=0)
        full_hidden = lax.all_gather(hidden, 'vocab', axis=0, tiled=True)
        own_scores = lax.dot_general(full_hidden, mine_rows, (((1,), (1,)), ((), ())), preferred_element_type=jnp.float32) * INV_TEMP
        return finish_rows(own_scores, owner_id, slot_rank, allowed_valid, target_pos, shards)

    row_spec = P(('rep', 'vocab'))
    mat_spec = P(('rep', 'vocab'), None)
    return jax.shard_map(device_step, mesh=mesh, in_specs=(mat_spec, P('vocab', None), P('rep'), P('rep'), row_spec), out_specs=(mat_spec, row_spec), check_vma=False)
```

profile of v0, /device:TPU:112, one launch (start us, length us, event | category | flops | bytes accessed | tf_op | source)
XLA Modules:
  0.0 290.0 jit_solution(8502141002647839538)
XLA Ops:
  7.2 0.1 all-gather.2.cloned.1.call-start
  7.2 0.7 all-gather.2.cloned.1.call-update
  8.0 0.7 add_select_fusion
  8.7 14.7 %scatter_custom_fusion = s32[8]{0:T(128)S(1)} fusion(s32[2048]{0:T(1024)S(1)} %get-tuple-element.15, s32[2048]{0:T(1024)S(1)} %ne.14, s32[]{:T(128)} %constant.20.clone.1), kind=kCustom, calls=%fused_computation.44 | custom fusion | flops 2048 | bytes 36 | tf_op jit(solution)/shard_map/scatter-add | solution.py:12
  23.4 0.2 reduce-window.9
  23.6 0.7 fusion.13
  25.5 5.0 %sort.34 = (s32[2048]{0:T(1024)}, s32[2048]{0:T(1024)S(1)}) sort(s32[2048]{0:T(1024)S(1)} %get-tuple-element.14, s32[2048]{0:T(1024)S(1)} %iota.8), dimensions={0}, to_apply=%region_0.1 | sort | flops 22528 | bytes 32768 | tf_op jit(solution)/shard_map/jit(argsort)/sort | solution.py:11
  31.1 0.1 compare_select_fusion.5
  31.2 3.4 %gather_fusion = s32[512]{0:T(512)S(1)} fusion(s32[2048]{0:T(1024)} %param.7, s32[1024]{0:T(1024)S(1)} %pad_clamp_fusion.1), kind=kCustom, calls=%fused_computation | custom fusion | bytes 6144 | tf_op jit(solution)/shard_map/gather | solution.py:17
  34.6 21.8 %gather_fusion.1 = bf16[512,2304]{1,0:T(8,128)(2,1)S(1)} fusion(bf16[32000,2304]{1,0:T(8,128)(2,1)} %param.6, s32[1024]{0:T(1024)S(1)} %pad_clamp_fusion), kind=kCustom, calls=%fused_computation.1 | custom fusion | bytes 4720640 | tf_op jit(solution)/shard_map/jit(_take)/gather | solution.py:42
  56.4 46.1 %all-gather.2.cloned.1.call-done = bf16[4096,2304]{1,0:T(8,128)(2,1)} async-done(((bf16[512,2304]{1,0:T(8,128)(2,1)}), bf16[4096,2304]{1,0:T(8,128)(2,1)}) %all-gather.2.cloned.1.call-update) | async-done | bytes 18874384 | tf_op jit(solution)/shard_map/all_gather | solution.py:43
  102.5 16.1 %convolution_multiply_fusion = f32[512,4096]{1,0:T(8,128)} fusion(bf16[4096,2304]{1,0:T(8,128)(2,1)} %all-gather.2.cloned.1.call-done, bf16[512,2304]{1,0:T(8,128)(2,1)S(1)} %gather_fusion.1, pred[512]{0:T(512)(128)(4,1)S(1)} %get-tuple-element.12), kind=kOutput, calls=%fused_computation.6 | convolution fusion | flops 9666953216 | bytes 29622784 | tf_op jit(solution)/shard_map/dot_general | solution.py:44
  118.5 8.0 %copy.13 = f32[64,8,8,512]{3,2,0,1:T(8,128)} copy(f32[64,8,8,512]{3,2,1,0:T(8,128)} %bitcast.31) | data formatting | bytes 16777216 | tf_op jit(solution)/shard_map/reshape | solution.py:23
  126.5 0.0 copy-start.3
  126.5 0.0 copy-start.2
  126.5 0.0 copy-start
  126.5 5.5 %all-to-all-start = ((f32[8,512,512]{1,2,0:T(8,128)}), f32[8,512,512]{1,2,0:T(8,128)}, u32[]{:S(2)}, u32[]{:S(2)}) async-start(f32[8,512,512]{1,2,0:T(8,128)} %bitcast.30), calls=%async_computation | async-start | bytes 16777216 | tf_op jit(solution)/shard_map/all_to_all | solution.py:24
  132.1 5.0 %sort.35 = (s32[2048]{0:T(1024)}, s32[2048]{0:T(1024)S(1)}) sort(s32[2048]{0:T(1024)S(1)} %get-tuple-element.4, s32[2048]{0:T(1024)S(1)} %iota.9), dimensions={0}, to_apply=%region_3.4 | sort | flops 22528 | bytes 32768 | tf_op jit(solution)/shard_map/jit(argsort)/sort | solution.py:14
  137.1 0.0 copy-done.3
  137.2 0.0 copy-done.2
  137.2 0.0 copy-done
  137.2 4.9 %fusion.5 = s32[2048]{0:T(1024)S(1)} fusion(s32[2048]{0:T(1024)S(1)} %get-tuple-element.5, s32[]{:T(128)} %bitcast.6, s32[]{:T(128)} %bitcast.7, s32[]{:T(128)} %bitcast.8, s32[]{:T(128)} %bitcast.9, s32[]{:T(128)} %bitcast.10, s32[]{:T(128)} %bitcast.11, s32[]{:T(128)} %bitcast.12, s32[]{:T(128)} %bitcast.13, s32[2048]{0:T(1024)S(1)} %copy-done), kind=kLoop, calls=%fused_computation.20 | loop fusion | flops 69632 | bytes 24608 | tf_op jit(solution)/shard_map/concatenate | solution.py:25
  142.1 84.1 %all-to-all-done = f32[8,512,512]{1,2,0:T(8,128)} async-done(((f32[8,512,512]{1,2,0:T(8,128)}), f32[8,512,512]{1,2,0:T(8,128)}, u32[]{:S(2)}, u32[]{:S(2)}) %all-to-all-start) | async-done | bytes 8388640 | tf_op jit(solution)/shard_map/all_to_all | solution.py:24
  226.3 35.6 %gather_fusion.2 = f32[2048,512]{1,0:T(8,128)} fusion(f32[8,512,512]{1,2,0:T(8,128)} %all-to-all-done, s32[2048]{0:T(1024)S(1)} %fusion.5), kind=kCustom, calls=%fused_computation.2 | custom fusion | bytes 8404992 | tf_op jit(solution)/shard_map/gather | solution.py:25
  261.9 0.0 copy-start.1
  261.9 2.6 select_reduce_fusion
  264.5 0.8 copy-done.1
  265.3 0.9 exponential_reduce_fusion
  266.2 7.1 %gather_fusion.3 = f32[512]{0:T(512)S(1)} fusion(f32[512,2048]{0,1:T(8,128)} %bitcast.28, s32[512]{0:T(512)S(1)} %bitcast.29), kind=kCustom, calls=%fused_computation.3 | custom fusion | bytes 8192 | tf_op jit(solution)/shard_map/jit(take_along_axis)/gather | solution.py:30
  273.3 0.6 select_subtract_fusion.1
  273.9 4.0 %exponential_select_fusion = f32[512,2048]{0,1:T(8,128)} fusion(f32[512]{0:T(512)S(1)} %get-tuple-element.11, pred[2048]{0:T(1024)(128)(4,1)S(1)} %broadcast_compare_fusion, f32[2048,512]{1,0:T(8,128)} %gather_fusion.2), kind=kLoop, calls=%fused_computation.7 | loop fusion | flops 3145728 | bytes 8392704 | tf_op jit(solution)/shard_map/jit(_where)/select_n | solution.py:29
  277.8 5.3 %copy.10 = f32[512,2048]{1,0:T(8,128)} copy(f32[512,2048]{0,1:T(8,128)} %exponential_select_fusion) | data formatting | bytes 8388608
  (14 shorter events, 0.1 us)
Async XLA Ops:
  7.2 95.3 %all-gather.2.cloned.1.call-start = ((), (), s32[]{:S(2)}) async-start(), calls=%async_computation.1 | async-start | bytes 21233664 | tf_op jit(solution)/shard_map/all_gather | solution.py:43
  126.5 10.6 %copy-start.3 = (s32[512]{0:T(512)S(1)}, s32[512]{0:T(512)}, u32[]{:S(2)}) copy-start(s32[512]{0:T(512)} %param.9) | copy-start | bytes 6148
  126.5 10.6 %copy-start.2 = (s32[2048]{0:T(1024)S(1)}, s32[2048]{0:T(1024)}, u32[]{:S(2)}) copy-start(s32[2048]{0:T(1024)} %param.8) | copy-start | bytes 24580
  126.5 10.7 %copy-start = (s32[2048]{0:T(1024)S(1)}, s32[2048]{0:T(1024)}, u32[]{:S(2)}) copy-start(s32[2048]{0:T(1024)} %param.7) | copy-start | bytes 24580
  126.5 99.7 %all-to-all-start = ((f32[8,512,512]{1,2,0:T(8,128)}), f32[8,512,512]{1,2,0:T(8,128)}, u32[]{:S(2)}, u32[]{:S(2)}) async-start(f32[8,512,512]{1,2,0:T(8,128)} %bitcast.30), calls=%async_computation | async-start | bytes 16777216 | tf_op jit(solution)/shard_map/all_to_all | solution.py:24
  261.9 3.4 %copy-start.1 = (f32[2048,512]{1,0:T(8,128)S(1)}, f32[2048,512]{1,0:T(8,128)}, u32[]{:S(2)}) copy-start(f32[2048,512]{1,0:T(8,128)} %gather_fusion.2) | copy-start | bytes 12582916
Sparse Core Ops, SparseCore 0:
  9.6 92.8 all-gather.1
where the time goes:
time: 291 us; the launch traced here: 290 us
  waiting for transfers between devices  131 us (45%)
  local copies, waits for them, and re-layouts  82.7 us (28%)
  other arithmetic  38.7 us (13%)
  matrix products  16.1 us (6%)
  between operations  16 us (5%)
  starting transfers between devices  5.59 us (2%)
    all_to_all x1, waiting for transfers between devices, finish_rows(): incoming = lax.all_to_all(outgoing, 'vocab', 0, 0)  84.1 us
    all_gather x1, waiting for transfers between devices, device_step(): full_hidden = lax.all_gather(hidden, 'vocab', axis=0, tiled=True)  46.1 us
    gather x1, local copies, waits for them, and re-layouts, finish_rows(): scores = incoming[owner_id, :, slot_rank].T  35.6 us
    gather x1, local copies, waits for them, and re-layouts, device_step(): mine_rows = jnp.take(w_head, local_idx, axis=0)  21.8 us
    dot_general x1, matrix products, device_step(): lax.dot_general(full_hidden, mine_rows, (((1,), (1,)), ((), ())), preferr...  16.1 us
    scatter-add x1, other arithmetic, owner_layout(): counts = jnp.bincount(owner_id, length=shards)  14.7 us
    reshape x1, local copies, waits for them, and re-layouts, finish_rows(): outgoing = own_scores.reshape(shards, rows_dev, own_scores.shape[1])  8.01 us
    gather x1, local copies, waits for them, and re-layouts, finish_rows(): picked = jnp.take_along_axis(scores, target_pos[:, None], axis=1)[:, 0]  7.06 us
  transfers between devices with their start and end apart: 2, of which 2 were waited for; matrix products, arithmetic and copies ran while one was open for 19% of the time, Pallas kernels for 0%

commit v1 on v0

v1 whole, which is shorter than its diff:
```python
import jax
import jax.numpy as jnp
from jax import lax
from jax.sharding import PartitionSpec as P

INV_TEMP = 1.25


def solution(mesh):

    def device_step(hidden, w_head, allowed_ids, allowed_valid, target_pos):
        my_index = lax.axis_index('vocab')
        vocab_local = w_head.shape[0]
        local_idx = allowed_ids - my_index * vocab_local
        mine = (local_idx >= 0) & (local_idx < vocab_local)
        rows = jnp.take(w_head, jnp.clip(local_idx, 0, vocab_local - 1), axis=0)
        rows = jnp.where(mine[:, None], rows, jnp.zeros((), rows.dtype))
        part = lax.psum_scatter(rows, 'vocab', scatter_dimension=0, tiled=True)
        rows = lax.all_gather(part, 'vocab', axis=0, tiled=True)
        scores = lax.dot_general(hidden, rows, (((1,), (1,)), ((), ())), preferred_element_type=jnp.float32) * INV_TEMP
        keep_mask = (allowed_valid > 0)[None, :]
        masked = jnp.where(keep_mask, scores, -jnp.inf)
        log_norm = jax.nn.logsumexp(masked, axis=1)
        token_probs = jnp.where(keep_mask, jnp.exp(masked - log_norm[:, None]), 0.0)
        lane = lax.broadcasted_iota(jnp.int32, scores.shape, 1)
        picked = jnp.sum(jnp.where(lane == target_pos[:, None], scores, 0.0), axis=1)
        return token_probs, picked - log_norm

    row_spec = P(('rep', 'vocab'))
    mat_spec = P(('rep', 'vocab'), None)
    return jax.shard_map(device_step, mesh=mesh, in_specs=(mat_spec, P('vocab', None), P('rep'), P('rep'), row_spec), out_specs=(mat_spec, row_spec), check_vma=False)
```

time: 291 us -> 265 us (0.911)
  other arithmetic: 38.7 us -> 15.9 us
  local copies, waits for them, and re-layouts: 82.7 us -> 105 us
  waiting for transfers between devices: 131 us -> 119 us
  matrix products: 16.1 us -> 7.64 us
  starting transfers between devices: 5.59 us -> 0.13 us
    all_to_all x1 -> x0, waiting for transfers between devices: 84.1 us -> none  [finish_rows(): incoming = lax.all_to_all(outgoing, 'vocab', 0, 0)]
    reduce_scatter x0 -> x1, waiting for transfers between devices: none -> 67.4 us  [device_step(): part = lax.psum_scatter(rows, 'vocab', scatter_dimension=0, tiled=True)]
    gather x5 -> x1, local copies, waits for them, and re-layouts: 68.5 us -> 99.9 us  [device_step(): rows = jnp.take(w_head, jnp.clip(local_idx, 0, vocab_local - 1), axis=0)]
    scatter-add x1 -> x0, other arithmetic: 14.7 us -> none  [owner_layout(): counts = jnp.bincount(owner_id, length=shards)]
    sort x2 -> x0, other arithmetic: 10.1 us -> none  [the longest x1 5.04 us: owner_layout(): sort_order = jnp.argsort(owner_id, stable=True)]
    dot_general x1, matrix products: 16.1 us -> 7.64 us  [device_step(): lax.dot_general(hidden, rows, (((1,), (1,)), ((), ())), preferred_element...]
    reshape x1 -> x0, local copies, waits for them, and re-layouts: 8.01 us -> none  [finish_rows(): outgoing = own_scores.reshape(shards, rows_dev, own_scores.shape[1])]
    select_n x6 -> x3, other arithmetic: 4.76 us -> 12.4 us  [the longest x1 9.95 us: device_step(): rows = jnp.where(mine[:, None], rows, jnp.zeros((), rows.dtype))]
  transfers between devices with their start and end apart: 2 -> 2, of which waited for: 2 -> 2; matrix products, arithmetic and copies ran while one was open for 19% -> 0% of each run, Pallas kernels for 0% -> 0%
where the time goes in v1:
time: 265 us; the launch traced here: 262 us
  waiting for transfers between devices  119 us (45%)
  local copies, waits for them, and re-layouts  105 us (40%)
  other arithmetic  15.9 us (6%)
  between operations  14.1 us (5%)
  matrix products  7.64 us (3%)
    gather x1, local copies, waits for them, and re-layouts, device_step(): rows = jnp.take(w_head, jnp.clip(local_idx, 0, vocab_local - 1), axis=0)  99.9 us
    reduce_scatter x1, waiting for transfers between devices, device_step(): part = lax.psum_scatter(rows, 'vocab', scatter_dimension=0, tiled=True)  67.4 us
    all_gather x1, waiting for transfers between devices, device_step(): rows = lax.all_gather(part, 'vocab', axis=0, tiled=True)  51 us
    select_n x1, other arithmetic, device_step(): rows = jnp.where(mine[:, None], rows, jnp.zeros((), rows.dtype))  9.95 us
    dot_general x1, matrix products, device_step(): lax.dot_general(hidden, rows, (((1,), (1,)), ((), ())), preferred_element...  7.64 us
    unnamed x7, local copies, waits for them, and re-layouts  5.36 us
  transfers between devices with their start and end apart: 2, of which 2 were waited for; matrix products, arithmetic and copies ran while one was open for 0% of the time, Pallas kernels for 0%

profile of v1, /device:TPU:112, one launch (start us, length us, event | category | flops | bytes accessed | tf_op | source)
XLA Modules:
  0.0 261.7 jit_solution(9679055524056641009)
XLA Ops:
  7.2 0.0 copy-start
  7.2 0.1 reduce-scatter.2.cloned.1.call-start
  7.3 0.9 compare_and_fusion.1
  8.1 0.7 fusion.2
  8.8 99.9 %gather_fusion = bf16[2048,2304]{1,0:T(8,128)(2,1)} fusion(bf16[32000,2304]{1,0:T(8,128)(2,1)} %param.6, s32[2048]{0:T(1024)S(1)} %fusion.2), kind=kCustom, calls=%fused_computation | custom fusion | bytes 18882560 | tf_op jit(solution)/shard_map/jit(_take)/gather | solution.py:16
  108.7 9.9 %select_select_fusion = bf16[2048,2304]{1,0:T(8,128)(2,1)} fusion(bf16[2048,2304]{1,0:T(8,128)(2,1)} %gather_fusion, pred[2048]{0:T(1024)(128)(4,1)S(1)} %get-tuple-element.9, pred[2048]{0:T(1024)(128)(4,1)S(1)} %get-tuple-element.8), kind=kLoop, calls=%fused_computation.1 | loop fusion | flops 9437184 | bytes 18878464 | tf_op jit(solution)/shard_map/jit(_where)/select_n | solution.py:17
  118.7 0.0 copy-start.1
  118.7 0.1 reduce-scatter.2.cloned.1.call-update
  118.7 0.1 all-gather.2.cloned.1.call-start
  118.8 67.4 %reduce-scatter.2.cloned.1.call-done = bf16[256,2304]{1,0:T(8,128)(2,1)} async-done(((bf16[2048,2304]{1,0:T(8,128)(2,1)}), bf16[256,2304]{1,0:T(8,128)(2,1)}) %reduce-scatter.2.cloned.1.call-update) | async-done | bytes 1179664 | tf_op jit(solution)/shard_map/reduce_scatter | solution.py:18
  186.2 0.1 all-gather.2.cloned.1.call-update
  186.3 0.0 copy-done.1
  186.3 0.0 copy-start.2
  186.3 51.0 %all-gather.2.cloned.1.call-done = bf16[2048,2304]{1,0:T(8,128)(2,1)} async-done(((bf16[256,2304]{1,0:T(8,128)(2,1)}), bf16[2048,2304]{1,0:T(8,128)(2,1)}) %all-gather.2.cloned.1.call-update) | async-done | bytes 9437200 | tf_op jit(solution)/shard_map/all_gather | solution.py:19
  237.4 0.0 copy-done
  237.4 7.6 %fusion.1 = (f32[512]{0:T(512)S(1)}, f32[2048,512]{1,0:T(8,128)S(1)}) fusion(pred[2048]{0:T(1024)(128)(4,1)S(1)} %broadcast_compare_fusion, bf16[2048,2304]{1,0:T(8,128)(2,1)} %all-gather.2.cloned.1.call-done, bf16[512,2304]{1,0:T(8,128)(2,1)S(1)} %copy-done), kind=kOutput, calls=%fused_computation.8 | convolution fusion | flops 4834983424 | bytes 15994880 | tf_op jit(solution)/shard_map/dot_general | solution.py:20
  245.0 0.0 copy-done.2
  245.0 1.4 fusion
  246.4 0.6 fusion.3
  247.0 2.4 exponential_select_fusion
  249.5 5.3 %copy.7 = f32[512,2048]{1,0:T(8,128)} copy(f32[512,2048]{0,1:T(8,128)} %exponential_select_fusion) | data formatting | bytes 8388608
  (2 shorter events, 0.0 us)
Async XLA Ops:
  7.2 230.2 %copy-start = (bf16[512,2304]{1,0:T(8,128)(2,1)S(1)}, bf16[512,2304]{1,0:T(8,128)(2,1)}, u32[]{:S(2)}) copy-start(bf16[512,2304]{1,0:T(8,128)(2,1)} %param.5) | copy-start | bytes 7077892
  7.2 179.0 %reduce-scatter.2.cloned.1.call-start = ((), (), s32[]{:S(2)}) async-start(), calls=%async_computation.1 | async-start | bytes 10616832 | tf_op jit(solution)/shard_map/reduce_scatter | solution.py:18
  118.7 67.6 %copy-start.1 = (s32[2048]{0:T(1024)S(1)}, s32[2048]{0:T(1024)}, u32[]{:S(2)}) copy-start(s32[2048]{0:T(1024)} %param.8) | copy-start | bytes 24580
  118.7 118.6 %all-gather.2.cloned.1.call-start = ((), (), s32[]{:S(2)}) async-start(), calls=%async_computation.2 | async-start | bytes 10616832 | tf_op jit(solution)/shard_map/all_gather | solution.py:19
  186.3 58.7 %copy-start.2 = (s32[512]{0:T(512)S(1)}, s32[512]{0:T(512)}, u32[]{:S(2)}) copy-start(s32[512]{0:T(512)} %param.9) | copy-start | bytes 6148
Sparse Core Ops, SparseCore 0:
  118.8 67.3 reduce-scatter.1
  187.8 49.5 all-gather.1

commit v2 on v1

v2 whole, which is shorter than its diff:
```python
import functools

import jax
import jax.numpy as jnp
from jax import lax
from jax.experimental import pallas as pl
from jax.experimental.pallas import tpu as pltpu
from jax.sharding import PartitionSpec as P

INV_TEMP = 1.25
MESH = pl.DeviceIdType.MESH
CHUNK = 64
LAG = 2
GATHER = 32
PACK = 8
GROUP = 256
CUT = 384


def gather_kernel(shards, base_ref, sid_ref, w_ref, gbuf_ref, stage, pick, outb, in_sem, out_sem):
    v = lax.axis_index('vocab')
    vocab_local = w_ref.shape[0]
    half = gbuf_ref.shape[1]
    chip = v // 2

    def span(k):
        first = base_ref[k * (shards + 1) + v]
        count = base_ref[k * (shards + 1) + v + 1] - first
        slot0 = first - base_ref[k * (shards + 1) + 2 * chip]
        block0 = slot0 // GATHER
        blocks = jnp.where(count > 0, (slot0 + count + GATHER - 1) // GATHER - block0, 0)
        return first, count, slot0, block0, blocks

    spans = [span(0), span(1)]
    total = spans[0][4] + spans[1][4]

    def where_is(t):
        second = t >= spans[0][4]
        first, count, slot0, block0 = [jnp.where(second, spans[1][i], spans[0][i]) for i in range(4)]
        k = jnp.where(second, 1, 0)
        block = block0 + jnp.where(second, t - spans[0][4], t)
        lo = jnp.maximum(slot0 - block * GATHER, 0)
        hi = jnp.minimum(slot0 + count - block * GATHER, GATHER)
        src = k * half + first + block * GATHER - slot0
        return k, block, lo, hi, src

    def row_copy(group, s, b):
        return pltpu.make_async_copy(
            w_ref.at[pl.ds(pl.multiple_of(group * PACK, PACK), PACK), :],
            stage.at[b, pl.ds(pl.multiple_of(s * PACK, PACK), PACK), :],
            in_sem.at[b])

    def out_copy(t, b):
        k, block, _, _, _ = where_is(t)
        return pltpu.make_async_copy(
            outb.at[b], gbuf_ref.at[k, pl.ds(pl.multiple_of(block * GATHER, GATHER), GATHER), :], out_sem.at[b])

    lane = lax.broadcasted_iota(jnp.int32, (1, GATHER * PACK), 1)

    def issue(t, b):
        _, _, lo, hi, src = where_is(t)
        pick[b] = jnp.zeros((GATHER, GATHER * PACK), jnp.float32)

        def one(s, carry):
            local = sid_ref[src + s] - v * vocab_local
            group = local // PACK
            row_copy(group, s, b).start()
            pick[b, pl.ds(s, 1), :] = jnp.where(lane == s * PACK + local - group * PACK, 1.0, 0.0)
            return carry

        lax.fori_loop(lo, hi, one, 0)

    stage[...] = jnp.zeros_like(stage)

    @pl.when(total > 0)
    def _():
        issue(0, 0)

    def step(t, carry):
        b = lax.rem(t, 2)

        @pl.when(t + 1 < total)
        def _():
            issue(t + 1, 1 - b)

        _, _, lo, hi, _ = where_is(t)

        def one(s, c):
            row_copy(0, s, b).wait()
            return c

        lax.fori_loop(lo, hi, one, 0)

        @pl.when(t >= 2)
        def _():
            out_copy(t - 2, b).wait()

        outb[b] = jnp.dot(pick[b].astype(jnp.bfloat16), stage[b], preferred_element_type=jnp.float32).astype(jnp.bfloat16)
        out_copy(t, b).start()
        return carry

    lax.fori_loop(0, total, step, 0)

    @pl.when(total >= 2)
    def _():
        out_copy(total - 2, lax.rem(total, 2)).wait()

    @pl.when(total >= 1)
    def _():
        out_copy(total - 1, lax.rem(total + 1, 2)).wait()


def ring_kernel(shards, base_ref, rank_ref, hidden_ref, gbuf_ref, out_ref,
                hid, mine, other, land, merged, theirs, slot_of, shift,
                hid_sem, mine_sem, other_send, other_recv, ring_send, ring_recv, pair_send, pair_recv):
    chips = shards // 2
    half = gbuf_ref.shape[1]
    lag_rows = LAG * CHUNK
    n_own = half // CHUNK
    n_wire = n_own + (chips - 2) * LAG
    n_all = n_own + (chips - 1) * LAG
    max_delay = half // CHUNK + 1
    depth = mine.shape[1]
    v = lax.axis_index('vocab')
    core = lax.rem(v, 2)
    chip = v // 2
    partner = chip * 2 + 1 - core
    ahead = lax.rem(chip + 2 * core - 1 + chips, chips) * 2 + core
    behind = lax.rem(chip - 2 * core + 1 + chips, chips) * 2 + core

    barrier = pltpu.get_barrier_semaphore()
    for peer in (partner, ahead, behind):
        pl.semaphore_signal(barrier, inc=1, device_id={'vocab': peer}, device_id_type=MESH)

    def rows(e, n=CHUNK):
        return pl.ds(pl.multiple_of(e * CHUNK, CHUNK), n)

    hid_copy = pltpu.make_async_copy(hidden_ref, hid, hid_sem)

    def mine_copy(e):
        return pltpu.make_async_copy(gbuf_ref.at[core, rows(e), :], mine.at[rows(e), :], mine_sem.at[e])

    def other_copy(e):
        return pltpu.make_async_remote_copy(
            src_ref=gbuf_ref.at[1 - core, rows(e), :], dst_ref=other.at[rows(e), :],
            send_sem=other_send.at[e], recv_sem=other_recv.at[e], device_id={'vocab': partner}, device_id_type=MESH)

    def ring_copy(e):
        return pltpu.make_async_remote_copy(
            src_ref=merged.at[rows(e), :], dst_ref=land.at[rows(e), :],
            send_sem=ring_send.at[e], recv_sem=ring_recv.at[e], device_id={'vocab': ahead}, device_id_type=MESH)

    def pair_copy(e):
        return pltpu.make_async_remote_copy(
            src_ref=merged.at[rows(e), :], dst_ref=theirs.at[rows(e), :],
            send_sem=pair_send.at[e], recv_sem=pair_recv.at[e], device_id={'vocab': partner}, device_id_type=MESH)

    def start_mine(e, c):
        mine_copy(e).start()
        return c

    lax.fori_loop(0, n_own, start_mine, 0)
    hid_copy.start()

    def base(k, w):
        return base_ref[k * (shards + 1) + w]

    for k in range(2):
        rank = rank_ref[k]
        slots = jnp.zeros_like(rank)
        passed = jnp.int32(0)
        for hop in range(chips):
            owner = lax.rem(chip - (2 * k - 1) * hop + chips, chips)
            low, high = base(k, 2 * owner), base(k, 2 * owner + 2)
            slots += jnp.where((rank >= low) & (rank < high), rank + (passed - low), 0)
            passed += jnp.maximum(high - low, lag_rows)
        slot_of[k] = slots
    out_ref[...] = jnp.zeros_like(out_ref)

    pl.semaphore_wait(barrier, 3)
    ahead_of_use = 3
    for e in range(ahead_of_use):
        other_copy(e).start()

    chip_low = base(core, 2 * chip)
    own_pad = jnp.maximum(base(core, 2 * chip + 2) - chip_low, lag_rows)
    delay = (own_pad + CHUNK - 1) // CHUNK
    row = lax.broadcasted_iota(jnp.int32, (CHUNK, 2 * CHUNK), 0)
    col = lax.broadcasted_iota(jnp.int32, (CHUNK, 2 * CHUNK), 1)
    shift[...] = jnp.where(col == row + delay * CHUNK - own_pad, 1.0, 0.0).astype(jnp.bfloat16)
    mine_low = base(core, v) - chip_low
    mine_high = base(core, v + 1) - chip_low
    other_low = base(core, partner) - chip_low
    other_high = base(core, partner + 1) - chip_low

    def score(k, src, q, slots):
        part = src[pl.ds(pl.multiple_of(q * GROUP, GROUP), slots), :]
        s = lax.dot_general(hid[...], part, (((1,), (1,)), ((), ())), preferred_element_type=jnp.float32) * INV_TEMP
        top = s.astype(jnp.bfloat16)
        rest = s - top.astype(jnp.float32)
        mid = rest.astype(jnp.bfloat16)
        low = (rest - mid.astype(jnp.float32)).astype(jnp.bfloat16)
        slot = lax.broadcasted_iota(jnp.int32, (slots, half), 0) + q * GROUP
        place = jnp.where(slot == slot_of[k], 1.0, 0.0).astype(jnp.bfloat16)
        cols = pl.ds(pl.multiple_of(k * half, half), half)
        moved = (jnp.dot(top, place, preferred_element_type=jnp.float32)
                 + jnp.dot(mid, place, preferred_element_type=jnp.float32)
                 + jnp.dot(low, place, preferred_element_type=jnp.float32))
        out_ref[:, cols] = out_ref[:, cols] + moved

    per_group = GROUP // CHUNK

    def wait_theirs(first, count):
        def one(e, c):
            pair_copy(e).wait_recv()
            return c
        lax.fori_loop(first, first + count, one, 0)

    def step(e, carry):
        @pl.when(e + ahead_of_use < n_own)
        def _():
            other_copy(e + ahead_of_use).start()

        @pl.when(e < n_own)
        def _():
            mine_copy(e).wait()
            other_copy(e).wait_recv()

        @pl.when(e >= LAG)
        def _():
            ring_copy(e - LAG).wait_recv()

        slot = lax.broadcasted_iota(jnp.int32, (CHUNK, 1), 0) + e * CHUNK
        is_mine = (slot >= mine_low) & (slot < mine_high)
        is_other = (slot >= other_low) & (slot < other_high)
        e_own = jnp.minimum(e, n_own - 1)
        zero = jnp.zeros((), jnp.float32)
        for cut in range(depth // CUT):
            cols = pl.ds(cut * CUT, CUT)

            def pick(c, acc):
                part = land[rows(c), cols]
                return jnp.where(c == e - delay, part, acc[0]), jnp.where(c == e - delay + 1, part, acc[1])

            empty = jnp.zeros((CHUNK, CUT), land.dtype)
            first, second = lax.fori_loop(jnp.maximum(e - max_delay, 0), e - LAG + 1, pick, (empty, empty))
            forward = jnp.dot(shift[...], jnp.concatenate([first, second], axis=0), preferred_element_type=jnp.float32)
            from_mine = jnp.where(is_mine, mine[rows(e_own), cols].astype(jnp.float32), zero)
            from_other = jnp.where(is_other, other[rows(e_own), cols].astype(jnp.float32), zero)
            merged[rows(e), cols] = (from_mine + from_other + forward).astype(jnp.bfloat16)

        @pl.when(e < n_wire)
        def _():
            ring_copy(e).start()

        pair_copy(e).start()

        q = e // per_group - 1

        @pl.when((q >= 0) & (lax.rem(e, per_group) == 0))
        def _():
            @pl.when(q == 0)
            def _():
                hid_copy.wait()

            score(core, merged, q, GROUP)

        @pl.when((q >= 0) & (lax.rem(e, per_group) == per_group // 2))
        def _():
            wait_theirs(q * per_group, per_group)
            score(1 - core, theirs, q, GROUP)

        return carry

    lax.fori_loop(0, n_all, step, 0)

    own_done = 0
    their_done = 0
    for e in range(n_all):
        if e // per_group >= 1 and e % per_group == 0:
            own_done = e // per_group
        if e // per_group >= 1 and e % per_group == per_group // 2:
            their_done = e // per_group
    for q in range(own_done, pl.cdiv(n_all, per_group)):
        score(core, merged, q, min(GROUP, n_all * CHUNK - q * GROUP))
    for q in range(their_done, pl.cdiv(n_all, per_group)):
        count = min(per_group, n_all - q * per_group)
        wait_theirs(q * per_group, count)
        score(1 - core, theirs, q, count * CHUNK)

    def finish(e, c):
        @pl.when(e < n_own)
        def _():
            other_copy(e).wait_send()

        @pl.when(e < n_wire)
        def _():
            ring_copy(e).wait_send()

        pair_copy(e).wait_send()
        return c

    lax.fori_loop(0, n_all, finish, 0)


def softmax_kernel(s_ref, valid_ref, target_ref, probs_ref, logp_ref):
    s = s_ref[...]
    keep = valid_ref[...] > 0
    masked = jnp.where(keep, s, -jnp.inf)
    top = jnp.max(masked, axis=1, keepdims=True)
    lse = jnp.log(jnp.sum(jnp.exp(masked - top), axis=1, keepdims=True)) + top
    probs_ref[...] = jnp.where(keep, jnp.exp(masked - lse), 0.0)
    lane = lax.broadcasted_iota(jnp.int32, s.shape, 1)
    picked = jnp.sum(jnp.where(lane == target_ref[...], s, 0.0), axis=1, keepdims=True)
    logp_ref[...] = picked - lse


def solution(mesh):
    shards = mesh.shape['vocab']

    def device_step(hidden, w_head, allowed_ids, allowed_valid, target_pos):
        list_len = allowed_ids.shape[0]
        half = list_len // 2
        vocab_local, depth = w_head.shape
        rows_dev = hidden.shape[0]
        chips = shards // 2
        ids = allowed_ids.reshape(2, half)
        rank = jnp.sum((ids[:, :, None] < ids[:, None, :]).astype(jnp.int32), axis=1)
        at = lax.broadcasted_iota(jnp.int32, (2, half, half), 1)
        sorted_ids = jnp.sum(jnp.where(rank[:, None, :] == at, ids[:, None, :], 0), axis=2)
        edges = lax.broadcasted_iota(jnp.int32, (2, shards + 1, half), 1) * vocab_local
        base = jnp.sum((ids[:, None, :] < edges).astype(jnp.int32), axis=2).reshape(-1)

        gbuf = pl.pallas_call(
            functools.partial(gather_kernel, shards),
            out_shape=jax.ShapeDtypeStruct((2, half, depth), w_head.dtype),
            in_specs=[pl.BlockSpec(memory_space=pltpu.SMEM), pl.BlockSpec(memory_space=pltpu.SMEM), pl.BlockSpec(memory_space=pl.ANY)],
            out_specs=pl.BlockSpec(memory_space=pl.ANY),
            scratch_shapes=[
                pltpu.VMEM((2, GATHER * PACK, depth), w_head.dtype),
                pltpu.VMEM((2, GATHER, GATHER * PACK), jnp.float32),
                pltpu.VMEM((2, GATHER, depth), w_head.dtype),
                pltpu.SemaphoreType.DMA((2,)),
                pltpu.SemaphoreType.DMA((2,)),
            ],
            name='gather_rows',
        )(base, sorted_ids.reshape(-1), w_head)

        n_own = half // CHUNK
        n_wire = n_own + (chips - 2) * LAG
        n_all = n_own + (chips - 1) * LAG
        scores = pl.pallas_call(
            functools.partial(ring_kernel, shards),
            out_shape=jax.ShapeDtypeStruct((rows_dev, list_len), jnp.float32),
            in_specs=[pl.BlockSpec(memory_space=pltpu.SMEM), pl.BlockSpec(memory_space=pltpu.VMEM),
                      pl.BlockSpec(memory_space=pl.ANY), pl.BlockSpec(memory_space=pl.ANY)],
            out_specs=pl.BlockSpec(memory_space=pltpu.VMEM),
            scratch_shapes=[
                pltpu.VMEM((rows_dev, depth), hidden.dtype),
                pltpu.VMEM((half, depth), w_head.dtype),
                pltpu.VMEM((half, depth), w_head.dtype),
                pltpu.VMEM((n_wire * CHUNK, depth), w_head.dtype),
                pltpu.VMEM((n_all * CHUNK, depth), w_head.dtype),
                pltpu.VMEM((n_all * CHUNK, depth), w_head.dtype),
                pltpu.VMEM((2, 1, half), jnp.int32),
                pltpu.VMEM((CHUNK, 2 * CHUNK), jnp.bfloat16),
                pltpu.SemaphoreType.DMA,
                pltpu.SemaphoreType.DMA((n_own,)),
                pltpu.SemaphoreType.DMA((n_own,)),
                pltpu.SemaphoreType.DMA((n_own,)),
                pltpu.SemaphoreType.DMA((n_wire,)),
                pltpu.SemaphoreType.DMA((n_wire,)),
                pltpu.SemaphoreType.DMA((n_all,)),
                pltpu.SemaphoreType.DMA((n_all,)),
            ],
            compiler_params=pltpu.CompilerParams(collective_id=0, has_side_effects=True, vmem_limit_bytes=62 * 1024 * 1024),
            name='ring_scores',
        )(base, rank.reshape(2, 1, half), hidden, gbuf)

        tile = 128
        probs, logp = pl.pallas_call(
            softmax_kernel,
            grid=(rows_dev // tile,),
            out_shape=[jax.ShapeDtypeStruct((rows_dev, list_len), jnp.float32), jax.ShapeDtypeStruct((rows_dev, 1), jnp.float32)],
            in_specs=[pl.BlockSpec((tile, list_len), lambda i: (i, 0)), pl.BlockSpec((1, list_len), lambda i: (0, 0)),
                      pl.BlockSpec((tile, 1), lambda i: (i, 0))],
            out_specs=[pl.BlockSpec((tile, list_len), lambda i: (i, 0)), pl.BlockSpec((tile, 1), lambda i: (i, 0))],
            name='softmax',
        )(scores, allowed_valid.reshape(1, list_len), target_pos.reshape(rows_dev, 1))
        return probs, logp.reshape(rows_dev)

    row_spec = P(('rep', 'vocab'))
    mat_spec = P(('rep', 'vocab'), None)
    return jax.shard_map(device_step, mesh=mesh, in_specs=(mat_spec, P('vocab', None), P('rep'), P('rep'), row_spec), out_specs=(mat_spec, row_spec), check_vma=False)
```

time: 265 us -> 136 us (0.51)
  Pallas kernels: 0 us -> 127 us
  waiting for transfers between devices: 119 us -> 0 us
  local copies, waits for them, and re-layouts: 105 us -> 3.47 us
  between operations: 14.1 us -> 0.67 us
  other arithmetic: 15.9 us -> 4.01 us
  matrix products: 7.64 us -> 0 us
    pallas_call x0 -> x3, Pallas kernels: none -> 127 us  [the longest x1 104 us: device_step(): pl.pallas_call(functools.partial(ring_kernel, shards), out_shape=jax.Shap...]
    gather x1 -> x0, local copies, waits for them, and re-layouts: 99.9 us -> none  [device_step(): rows = jnp.take(w_head, jnp.clip(local_idx, 0, vocab_local - 1), axis=0)]
    reduce_scatter x1 -> x0, waiting for transfers between devices: 67.4 us -> none  [device_step(): part = lax.psum_scatter(rows, 'vocab', scatter_dimension=0, tiled=True)]
    all_gather x1 -> x0, waiting for transfers between devices: 51 us -> none  [device_step(): rows = lax.all_gather(part, 'vocab', axis=0, tiled=True)]
    select_n x3 -> x0, other arithmetic: 12.4 us -> none  [the longest x1 9.95 us: device_step(): rows = jnp.where(mine[:, None], rows, jnp.zeros((), rows.dtype))]
    dot_general x1 -> x0, matrix products: 7.64 us -> none  [device_step(): lax.dot_general(hidden, rows, (((1,), (1,)), ((), ())), preferred_element...]
    unnamed x7 -> x3, local copies, waits for them, and re-layouts: 5.36 us -> 0.61 us
  transfers between devices with their start and end apart: 2 -> 0, of which waited for: 2 -> 0; matrix products, arithmetic and copies ran while one was open for 0% -> 0% of each run, Pallas kernels for 0% -> 0%
where the time goes in v2:
time: 136 us; the launch traced here: 135 us
  Pallas kernels  127 us (93%)
  other arithmetic  4.01 us (3%)
  local copies, waits for them, and re-layouts  3.47 us (3%)
    pallas_call x1, Pallas kernels, device_step(): pl.pallas_call(functools.partial(ring_kernel, shards), out_shape=jax.Shap...  104 us
    pallas_call x1, Pallas kernels, device_step(): pl.pallas_call(functools.partial(gather_kernel, shards), out_shape=jax.Sh...  17.3 us
    pallas_call x1, Pallas kernels, device_step(): pl.pallas_call(softmax_kernel, grid=(rows_dev // tile,), out_shape=[jax.S...  5.85 us

profile of v2, /device:TPU:112, one launch (start us, length us, event | category | flops | bytes accessed | tf_op | source)
XLA Modules:
  0.0 135.1 jit_solution(4176287581724159887)
XLA Ops:
  0.6 0.7 lt.23
  1.3 1.0 convert_reduce_fusion
  2.3 1.0 select_reduce_fusion
  3.4 0.6 copy.12
  4.0 0.3 fusion
  4.3 0.1 copy.8
  4.4 0.6 reshape.25.base_ref
  5.0 17.3 %gather_rows.1.gbuf_ref = bf16[2,1024,2304]{2,1,0:T(8,128)(2,1)} custom-call(s32[18]{0:T(128)} %reshape.25.base_ref, s32[2048]{0:T(1024)} %bitcast.6, bf16[32000,2304]{1,0:T(8,128)(2,1)} %w_ref.1), custom_call_target="tpu_custom_call" | custom-call | tf_op jit(solution)/shard_map/gather_rows/pallas_call | solution.py:334
  22.3 0.0 copy-start
  22.3 0.6 reshape.26.rank_ref
  22.9 103.8 %ring_scores.1.s_ref = f32[512,2048]{1,0:T(8,128)} custom-call(s32[18]{0:T(128)} %reshape.25.base_ref, s32[2,1,1024]{2,1,0:T(1,128)} %reshape.26.rank_ref, bf16[512,2304]{1,0:T(8,128)(2,1)} %hidden_ref.1, bf16[2,1024,2304]{2,1,0:T(8,128)(2,1)} %gather_rows.1.gbuf_ref), custom_call_target="tpu_custom_call" | custom-call | tf_op jit(solution)/shard_map/ring_scores/pallas_call | solution.py:352
  126.7 0.0 copy-done
  126.7 0.8 copy.9.target_ref
  127.5 5.8 %softmax.1 = (f32[512,2048]{1,0:T(8,128)}, f32[512,1]{1,0:T(8,128)}) custom-call(f32[512,2048]{1,0:T(8,128)} %ring_scores.1.s_ref, s32[1,2048]{1,0:T(1,128)} %bitcast.8, s32[512,1]{1,0:T(8,128)} %copy.9.target_ref), custom_call_target="tpu_custom_call" | custom-call | tf_op jit(solution)/shard_map/softmax/pallas_call | solution.py:381
  133.4 1.7 %reduce = f32[512]{0:T(512)} reduce(f32[512,1]{1,0:T(8,128)} %get-tuple-element.5, f32[]{:T(128)} %constant.4), dimensions={1}, to_apply=%get-tuple-element.5.reduce_sub_computation | reduce | bytes 4100 | tf_op jit(solution)/shard_map/softmax/pallas_call | solution.py:381
  (1 shorter events, 0.0 us)
Async XLA Ops:
  22.3 104.4 %copy-start = (s32[512]{0:T(512)S(1)}, s32[512]{0:T(512)}, u32[]{:S(2)}) copy-start(s32[512]{0:T(512)} %param.9) | copy-start | bytes 6148
